TPU v7x, 32 devices: a whole 2x2x4 slice. The times are simulated.
32 devices in a mesh: img: 4 (over y, x), row: 8 (over z, core).
Axes of the slice: x: 2, y: 2, z: 4, core: 2. Of those that a mesh axis runs over, the one named last changes fastest.
Arguments:
- latent: bfloat16 [128, 128, 512], P(('img', 'row')), parts along dimension 0, may hold values from -8 to 8
- attn_gain: float32 [512], replicated, may hold values from 0.5 to 1.5
- attn_shift: float32 [512], replicated, may hold values from -3 to 3
- w_query: bfloat16 [512, 512], replicated, may hold values from -2 to 2
- w_key: bfloat16 [512, 512], replicated, may hold values from -2 to 2
- w_value: bfloat16 [512, 512], replicated, may hold values from -0.25 to 0.25
- w_out: bfloat16 [512, 512], replicated, may hold values from -0.25 to 0.25
- conv_gain: float32 [512], replicated, may hold values from 0.5 to 1.5
- conv_shift: float32 [512], replicated, may hold values from -3 to 3
- w_conv: bfloat16 [3, 3, 512, 512], replicated, may hold values from -0.09375 to 0.09375
- conv_bias: float32 [512], replicated, may hold values from -3 to 3
Outputs:
- encoded: bfloat16 [128, 128, 512], P(('img', 'row')), parts along dimension 0
There are 4 independent parts, one for each index of `img`. A program takes and returns all parts, laid end to end along the dimension named above; an argument that names none is the same for every part. Nothing has to cross between parts.
All inputs are finite; a program needn't handle non-finite values.
Results may differ from a plain program's by a relative error of at most 0.011.
Values may be sent and summed in bfloat16 or wider, within the bound.
A program may use at most 128 MiB of HBM per device.

v0:
```python
import functools
import math

import jax
import jax.numpy as jnp
from jax import lax
from jax.experimental import pallas as pl
from jax.experimental.pallas import tpu as pltpu
from jax.sharding import PartitionSpec as P

GROUPS = 32
EPS = 1e-06
CHUNK = 128
MESH = pl.DeviceIdType.MESH
LOG2E = math.log2(math.e)
NT = (((1,), (1,)), ((), ()))


def spread_groups(row, ones):
    high = row.astype(jnp.bfloat16).astype(jnp.float32)
    rest = row - high
    mid = rest.astype(jnp.bfloat16).astype(jnp.float32)
    low = rest - mid
    index = lax.broadcasted_iota(jnp.int32, (16, row.shape[1]), 0)
    parts = jnp.where(index == 0, high, jnp.where(index == 1, mid, jnp.where(index == 2, low, 0.0)))
    sums = jnp.dot(parts.astype(jnp.bfloat16), ones, preferred_element_type=jnp.float32)
    return jnp.sum(sums, axis=0, keepdims=True)


def kernel(
    n, wide,
    latent, w_query, w_key, w_value, w_out, w_conv,
    attn_gain, attn_shift, conv_gain, conv_shift, conv_bias,
    out,
    kv, wq, wk, wv, wo, wc, ones, moments, queries, bias, maxima, total, acc, hidden, halo, stacked,
    load_sem, weight_sem, send_sem, recv_sem, stat_send, stat_recv, halo_send, halo_recv,
    result, store_sem,
):
    chunks, chunk, channels = kv.shape[1:]
    rows = chunks * chunk
    deep = n // 2
    lines = rows // wide
    size = channels // GROUPS
    img = lax.axis_index("img")
    r = lax.axis_index("row")
    z = r // 2
    c = r % 2
    partner = r + 1 - 2 * c

    loads = [
        pltpu.make_async_copy(latent.at[k], kv.at[r, k], load_sem.at[k]) for k in range(chunks)
    ]
    for load in loads:
        load.start()
    weights = [
        pltpu.make_async_copy(source, target, weight_sem.at[i])
        for i, (source, target) in enumerate([(w_query, wq), (w_key, wk), (w_value, wv), (w_out, wo)])
    ]
    weights += [
        pltpu.make_async_copy(
            w_conv.at[dy, dx],
            wc.at[dx, pl.ds(dy * channels, channels)],
            weight_sem.at[4 + dy * 3 + dx],
        )
        for dy in range(3)
        for dx in range(3)
    ]
    for weight in weights:
        weight.start()

    barrier = pltpu.get_barrier_semaphore()

    @pl.loop(1, n)
    def _(j):
        pl.semaphore_signal(
            barrier, inc=1, device_id=(img, lax.rem(r + j, n)), device_id_type=MESH
        )

    def piece(way, zb, k):
        b = zb * 2 + c
        target = (r + 2, r - 2, partner)[way]
        return pltpu.make_async_remote_copy(
            src_ref=kv.at[b, k],
            dst_ref=kv.at[b, k],
            send_sem=send_sem.at[way, zb, k],
            recv_sem=recv_sem.at[b, k],
            device_id=(img, target),
            device_id_type=MESH,
        )

    def arrival(b, k):
        return pltpu.make_async_remote_copy(
            src_ref=kv.at[b, k],
            dst_ref=kv.at[b, k],
            send_sem=send_sem.at[0, 0, 0],
            recv_sem=recv_sem.at[b, k],
            device_id=(img, partner),
            device_id_type=MESH,
        )

    def stat_copy(which, j):
        return pltpu.make_async_remote_copy(
            src_ref=moments.at[which, r],
            dst_ref=moments.at[which, r],
            send_sem=stat_send.at[which, j],
            recv_sem=stat_recv.at[which, r],
            device_id=(img, lax.rem(r + j, n)),
            device_id_type=MESH,
        )

    def stat_arrival(which, b):
        return pltpu.make_async_remote_copy(
            src_ref=moments.at[which, b],
            dst_ref=moments.at[which, b],
            send_sem=stat_send.at[which, 0],
            recv_sem=stat_recv.at[which, b],
            device_id=(img, partner),
            device_id_type=MESH,
        )

    def send_own(k):
        @pl.when(z < deep - 1)
        def _():
            piece(0, z, k).start()

        @pl.when(z > 0)
        def _():
            piece(1, z, k).start()

        piece(2, z, k).start()

    def share_moments(which, field):
        mean = jnp.sum(field, axis=0, keepdims=True) * (1.0 / rows)
        offset = field - mean
        square = jnp.sum(offset * offset, axis=0, keepdims=True)
        moments[which, r, 0:1, :] = mean
        moments[which, r, 1:2, :] = square

        @pl.loop(1, n)
        def _(j):
            stat_copy(which, j).start()

    def gather_moments(which):
        @pl.loop(1, n)
        def _(j):
            stat_arrival(which, lax.rem(r + j, n)).wait_recv()

        @pl.loop(1, n)
        def _(j):
            stat_copy(which, j).wait_send()

        every = moments[which]
        means = every[:, 0, :]
        squares = every[:, 1, :]
        centre = spread_groups(jnp.sum(means, axis=0, keepdims=True), ones[...]) * (
            1.0 / (n * size)
        )
        away = means - centre
        whole = jnp.sum(squares + rows * (away * away), axis=0, keepdims=True)
        variance = spread_groups(whole, ones[...]) * (1.0 / (n * size * rows))
        return centre, lax.rsqrt(variance + EPS)

    for load in loads:
        load.wait()
    pl.semaphore_wait(barrier, n - 1)
    send_own(0)
    share_moments(0, kv[r].reshape(rows, channels).astype(jnp.float32))
    for k in range(1, chunks):
        send_own(k)

    left_group = lax.broadcasted_iota(jnp.int32, (channels, channels), 0) // size
    right_group = lax.broadcasted_iota(jnp.int32, (channels, channels), 1) // size
    ones[...] = jnp.where(left_group == right_group, 1.0, 0.0).astype(jnp.bfloat16)
    maxima[...] = jnp.full_like(maxima, -1e30)
    total[...] = jnp.zeros_like(total)
    acc[...] = jnp.zeros_like(acc)

    for weight in weights[:2]:
        weight.wait()
    centre, scale = gather_moments(0)
    gain = scale * attn_gain[...]
    positions = kv[r].reshape(rows, channels).astype(jnp.float32)
    normed = ((positions - centre) * gain + attn_shift[...]).astype(jnp.bfloat16)
    query = jnp.dot(normed, wq[...], preferred_element_type=jnp.float32).astype(jnp.bfloat16)
    folded = lax.dot_general(query, wk[...], NT, preferred_element_type=jnp.float32) * (
        LOG2E / math.sqrt(channels)
    )
    queries[...] = (folded * gain).astype(jnp.bfloat16)
    constant = jnp.sum(folded * (attn_shift[...] - centre * gain), axis=1, keepdims=True)
    bias[...] = jnp.broadcast_to(constant, bias.shape)

    def attend(b, k):
        block = kv[b, k]
        scores = lax.dot_general(queries[...], block, NT, preferred_element_type=jnp.float32)
        scores = scores + jnp.tile(bias[...], (1, chunk // 128))
        newest = jnp.maximum(maxima[...], jnp.max(scores, axis=1, keepdims=True))
        fade = jnp.exp2(maxima[...] - newest)
        maxima[...] = newest
        probs = jnp.exp2(scores - jnp.tile(newest, (1, chunk // 128))).astype(jnp.bfloat16)
        kept = probs.astype(jnp.float32)
        summed = total[...] * fade
        for j in range(chunk // 128):
            summed = summed + kept[:, j * 128 : (j + 1) * 128]
        total[...] = summed
        product = jnp.dot(probs, block, preferred_element_type=jnp.float32)
        acc[...] = acc[...] * jnp.tile(fade, (1, channels // 128)) + product

    def relay(t):
        d = t // chunks
        k = t % chunks
        for way, zb in ((0, z - d), (1, z + d)):
            inside = jnp.logical_and(d > 0, jnp.logical_and(zb >= 0, zb < deep))

            @pl.when(inside)
            def _(way=way, zb=zb):
                arrival(zb * 2 + c, k).wait_recv()

                @pl.when((z < deep - 1) if way == 0 else (z > 0))
                def _():
                    piece(way, zb, k).start()

                piece(2, zb, k).start()

    ahead = jnp.where(jnp.logical_and(z > 0, z < deep - 1), chunks, 0)

    @pl.loop(0, deep * chunks)
    def _(t):
        relay(t + ahead)
        d = t // chunks
        k = t % chunks

        @pl.loop(0, 4)
        def _(j):
            side = j % 2
            other = j // 2
            zb = z + d * (2 * side - 1)
            inside = jnp.logical_and(zb >= 0, zb < deep)

            @pl.when(jnp.logical_and(inside, jnp.logical_or(side == 0, d > 0)))
            def _():
                b = zb * 2 + c + other * (1 - 2 * c)

                @pl.when(other == 1)
                def _():
                    arrival(b, k).wait_recv()

                attend(b, k)

    for weight in weights[2:4]:
        weight.wait()
    denominator = jnp.sum(total[...], axis=1, keepdims=True)
    average = (acc[...] / denominator - centre) * gain + attn_shift[...]
    attended = jnp.dot(
        average.astype(jnp.bfloat16), wv[...], preferred_element_type=jnp.float32
    ).astype(jnp.bfloat16)
    field = (
        kv[r].reshape(rows, channels).astype(jnp.float32)
        + jnp.dot(attended, wo[...], preferred_element_type=jnp.float32)
    ).astype(jnp.bfloat16)
    hidden[...] = field
    share_moments(1, field.astype(jnp.float32))

    up = pltpu.make_async_remote_copy(
        src_ref=hidden.at[pl.ds(0, wide)],
        dst_ref=halo.at[1],
        send_sem=halo_send.at[1],
        recv_sem=halo_recv.at[1],
        device_id=(img, r - 1),
        device_id_type=MESH,
    )
    down = pltpu.make_async_remote_copy(
        src_ref=hidden.at[pl.ds(rows - wide, wide)],
        dst_ref=halo.at[0],
        send_sem=halo_send.at[0],
        recv_sem=halo_recv.at[0],
        device_id=(img, r + 1),
        device_id_type=MESH,
    )

    @pl.when(r > 0)
    def _():
        up.start()

    @pl.when(r < n - 1)
    def _():
        down.start()

    @pl.loop(0, deep * chunks)
    def _(t):
        zb = t // chunks
        k = t % chunks

        @pl.when(jnp.logical_and(z < deep - 1, zb <= z))
        def _():
            piece(0, zb, k).wait_send()

        @pl.when(jnp.logical_and(z > 0, zb >= z))
        def _():
            piece(1, zb, k).wait_send()

        piece(2, zb, k).wait_send()

    for weight in weights[4:]:
        weight.wait()
    centre, scale = gather_moments(1)
    gain = scale * conv_gain[...]

    def activate(values):
        v = (values.astype(jnp.float32) - centre) * gain + conv_shift[...]
        return (v / (1.0 + jnp.exp(-v))).astype(jnp.bfloat16)

    def place(line, values):
        for dy in range(3):
            y = line + 1 - dy
            if 0 <= y < lines:
                stacked[y * wide : (y + 1) * wide, dy * channels : (dy + 1) * channels] = values

    for line in range(lines):
        place(line, activate(hidden[line * wide : (line + 1) * wide]))

    @pl.when(r > 0)
    def _():
        up.wait_send()
        down.wait_recv()
        place(-1, activate(halo[0]))

    @pl.when(r == 0)
    def _():
        place(-1, jnp.zeros((wide, channels), jnp.bfloat16))

    @pl.when(r < n - 1)
    def _():
        down.wait_send()
        up.wait_recv()
        place(lines, activate(halo[1]))

    @pl.when(r == n - 1)
    def _():
        place(lines, jnp.zeros((wide, channels), jnp.bfloat16))

    half = 256
    stores = []
    column = lax.broadcasted_iota(jnp.int32, (rows, half), 0) % wide
    for start in range(0, channels, half):
        cut = slice(start, start + half)

        def taps(dx):
            return jnp.dot(stacked[...], wc[dx, :, cut], preferred_element_type=jnp.float32)

        convolved = taps(1)
        convolved = convolved + jnp.where(column > 0, pltpu.roll(taps(0), 1, 0), 0.0)
        convolved = convolved + jnp.where(
            column < wide - 1, pltpu.roll(taps(2), rows - 1, 0), 0.0
        )
        encoded = hidden[:, cut].astype(jnp.float32) + (convolved + conv_bias[:, cut])
        result[:, cut] = encoded.astype(jnp.bfloat16)
        store = pltpu.make_async_copy(
            result.at[:, cut], out.at[:, cut], store_sem.at[start // half]
        )
        store.start()
        stores.append(store)

    for store in stores:
        store.wait()


def local(n, latent, attn_gain, attn_shift, w_query, w_key, w_value, w_out,
          conv_gain, conv_shift, w_conv, conv_bias):
    height, wide, channels = latent.shape
    rows = height * wide
    chunks = rows // CHUNK
    anywhere = pl.BlockSpec(memory_space=pl.ANY)
    vmem = pl.BlockSpec(memory_space=pltpu.VMEM)
    bf16, f32 = jnp.bfloat16, jnp.float32
    square = pltpu.VMEM((channels, channels), bf16)
    dma = pltpu.SemaphoreType.DMA
    encoded = pl.pallas_call(
        functools.partial(kernel, n, wide),
        out_shape=jax.ShapeDtypeStruct((rows, channels), bf16),
        in_specs=[anywhere] * 6 + [vmem] * 5,
        out_specs=anywhere,
        scratch_shapes=[
            pltpu.VMEM((n, chunks, CHUNK, channels), bf16),
            square, square, square, square,
            pltpu.VMEM((3, 3 * channels, channels), bf16),
            square,
            pltpu.VMEM((2, n, 2, channels), f32),
            pltpu.VMEM((rows, channels), bf16),
            pltpu.VMEM((rows, 128), f32),
            pltpu.VMEM((rows, 128), f32),
            pltpu.VMEM((rows, 128), f32),
            pltpu.VMEM((rows, channels), f32),
            pltpu.VMEM((rows, channels), bf16),
            pltpu.VMEM((2, wide, channels), bf16),
            pltpu.VMEM((rows, 3 * channels), bf16),
            dma((chunks,)),
            dma((13,)),
            dma((3, n // 2, chunks)),
            dma((n, chunks)),
            dma((2, n)),
            dma((2, n)),
            dma((2,)),
            dma((2,)),
            pltpu.VMEM((rows, channels), bf16),
            dma((channels // 256,)),
        ],
        compiler_params=pltpu.CompilerParams(
            collective_id=0, has_side_effects=True, vmem_limit_bytes=56 * 1024 * 1024
        ),
    )(
        latent.reshape(chunks, CHUNK, channels), w_query, w_key, w_value, w_out, w_conv,
        *(v.reshape(1, channels) for v in (attn_gain, attn_shift, conv_gain, conv_shift, conv_bias)),
    )
    return encoded.reshape(height, wide, channels)


def solution(mesh):
    in_specs = (P(("img", "row"), None, None), P(), P(), P(), P(), P(), P(), P(), P(), P(), P())
    out_specs = P(("img", "row"), None, None)
    body = functools.partial(local, mesh.shape["row"])
    return jax.shard_map(body, mesh=mesh, in_specs=in_specs, out_specs=out_specs, check_vma=False)
```

profile of v0, /device:TPU:0, one launch (start us, length us, event | category | flops | bytes accessed | tf_op | source)
XLA Modules:
  0.0 55.8 jit_solution(1826381401670771165)
XLA Ops:
  0.0 53.9 %shard_map.109 = bf16[512,512]{1,0:T(8,128)(2,1)} custom-call(bf16[4,128,512]{2,1,0:T(8,128)(2,1)} %latent.1, bf16[512,512]{1,0:T(8,128)(2,1)} %w_query.1, bf16[512,512]{1,0:T(8,128)(2,1)} %w_key.1, bf16[512,512]{1,0:T(8,128)(2,1)} %w_value.1, bf16[512,512]{1,0:T(8,128)(2,1)} %w_out.1, bf16[3,3,512,512]{3,2,1,0:T(8,128)(2,1)} %w_conv.1, f32[1,512]{1,0:T(1,128)} %bitcast.7, ...), custom_call_target="tpu_custom_call" | custom-call | tf_op jit(solution)/shard_map/pallas_call | solution.py:377
  53.9 1.9 %copy.13 = bf16[4,128,512]{2,1,0:T(8,128)(2,1)} copy(bf16[4,128,512]{2,1,0:T(8,128)(2,1)} %bitcast.6) | data formatting | bytes 1048576
where the time goes:
time: 56 us; the launch traced here: 55.8 us
  Pallas kernels  53.9 us (96%)
  local copies, waits for them, and re-layouts  1.87 us (3%)
    pallas_call x1, Pallas kernels, local(): pl.pallas_call(functools.partial(kernel, n, wide), out_shape=jax.ShapeDty...  53.9 us
    unnamed x1, local copies, waits for them, and re-layouts  1.87 us

commit v1 on v0

--- a/solution.py
+++ b/solution.py
@@ -11,6 +11,7 @@
 GROUPS = 32
 EPS = 1e-06
 CHUNK = 128
+BAND = 256
 MESH = pl.DeviceIdType.MESH
 LOG2E = math.log2(math.e)
 NT = (((1,), (1,)), ((), ()))
@@ -34,9 +35,8 @@
     out,
     kv, wq, wk, wv, wo, wc, ones, moments, queries, bias, maxima, total, acc, hidden, halo, stacked,
     load_sem, weight_sem, send_sem, recv_sem, stat_send, stat_recv, halo_send, halo_recv,
-    result, store_sem,
 ):
-    chunks, chunk, channels = kv.shape[1:]
+    chunks, cores, chunk, channels = kv.shape[1:]
     rows = chunks * chunk
     deep = n // 2
     lines = rows // wide
@@ -48,7 +48,7 @@
     partner = r + 1 - 2 * c
 
     loads = [
-        pltpu.make_async_copy(latent.at[k], kv.at[r, k], load_sem.at[k]) for k in range(chunks)
+        pltpu.make_async_copy(latent.at[k], kv.at[z, k, c], load_sem.at[k]) for k in range(chunks)
     ]
     for load in loads:
         load.start()
@@ -65,8 +65,6 @@
         for dy in range(3)
         for dx in range(3)
     ]
-    for weight in weights:
-        weight.start()
 
     barrier = pltpu.get_barrier_semaphore()
 
@@ -77,23 +75,22 @@
         )
 
     def piece(way, zb, k):
-        b = zb * 2 + c
         target = (r + 2, r - 2, partner)[way]
         return pltpu.make_async_remote_copy(
-            src_ref=kv.at[b, k],
-            dst_ref=kv.at[b, k],
+            src_ref=kv.at[zb, k, c],
+            dst_ref=kv.at[zb, k, c],
             send_sem=send_sem.at[way, zb, k],
-            recv_sem=recv_sem.at[b, k],
+            recv_sem=recv_sem.at[zb, k, c],
             device_id=(img, target),
             device_id_type=MESH,
         )
 
-    def arrival(b, k):
+    def arrival(zb, k, core):
         return pltpu.make_async_remote_copy(
-            src_ref=kv.at[b, k],
-            dst_ref=kv.at[b, k],
+            src_ref=kv.at[zb, k, core],
+            dst_ref=kv.at[zb, k, core],
             send_sem=send_sem.at[0, 0, 0],
-            recv_sem=recv_sem.at[b, k],
+            recv_sem=recv_sem.at[zb, k, core],
             device_id=(img, partner),
             device_id_type=MESH,
         )
@@ -118,6 +115,9 @@
             device_id_type=MESH,
         )
 
+    def own_rows():
+        return kv[z, :, c].reshape(rows, channels)
+
     def send_own(k):
         @pl.when(z < deep - 1)
         def _():
@@ -160,13 +160,18 @@
         variance = spread_groups(whole, ones[...]) * (1.0 / (n * size * rows))
         return centre, lax.rsqrt(variance + EPS)
 
-    for load in loads:
-        load.wait()
-    pl.semaphore_wait(barrier, n - 1)
-    send_own(0)
-    share_moments(0, kv[r].reshape(rows, channels).astype(jnp.float32))
-    for k in range(1, chunks):
-        send_own(k)
+    with jax.named_scope("load"):
+        for load in loads:
+            load.wait()
+    for weight in weights:
+        weight.start()
+    with jax.named_scope("barrier"):
+        pl.semaphore_wait(barrier, n - 1)
+    with jax.named_scope("share0"):
+        send_own(0)
+        share_moments(0, own_rows().astype(jnp.float32))
+        for k in range(1, chunks):
+            send_own(k)
 
     left_group = lax.broadcasted_iota(jnp.int32, (channels, channels), 0) // size
     right_group = lax.broadcasted_iota(jnp.int32, (channels, channels), 1) // size
@@ -175,11 +180,14 @@
     total[...] = jnp.zeros_like(total)
     acc[...] = jnp.zeros_like(acc)
 
-    for weight in weights[:2]:
+    for weight in weights[:4]:
         weight.wait()
-    centre, scale = gather_moments(0)
+    with jax.named_scope("fold"):
+        wv[...] = jnp.dot(wv[...], wo[...], preferred_element_type=jnp.float32).astype(jnp.bfloat16)
+    with jax.named_scope("stat0"):
+        centre, scale = gather_moments(0)
     gain = scale * attn_gain[...]
-    positions = kv[r].reshape(rows, channels).astype(jnp.float32)
+    positions = own_rows().astype(jnp.float32)
     normed = ((positions - centre) * gain + attn_shift[...]).astype(jnp.bfloat16)
     query = jnp.dot(normed, wq[...], preferred_element_type=jnp.float32).astype(jnp.bfloat16)
     folded = lax.dot_general(query, wk[...], NT, preferred_element_type=jnp.float32) * (
@@ -189,21 +197,26 @@
     constant = jnp.sum(folded * (attn_shift[...] - centre * gain), axis=1, keepdims=True)
     bias[...] = jnp.broadcast_to(constant, bias.shape)
 
-    def attend(b, k):
-        block = kv[b, k]
-        scores = lax.dot_general(queries[...], block, NT, preferred_element_type=jnp.float32)
-        scores = scores + jnp.tile(bias[...], (1, chunk // 128))
-        newest = jnp.maximum(maxima[...], jnp.max(scores, axis=1, keepdims=True))
-        fade = jnp.exp2(maxima[...] - newest)
-        maxima[...] = newest
-        probs = jnp.exp2(scores - jnp.tile(newest, (1, chunk // 128))).astype(jnp.bfloat16)
-        kept = probs.astype(jnp.float32)
-        summed = total[...] * fade
-        for j in range(chunk // 128):
-            summed = summed + kept[:, j * 128 : (j + 1) * 128]
-        total[...] = summed
-        product = jnp.dot(probs, block, preferred_element_type=jnp.float32)
-        acc[...] = acc[...] * jnp.tile(fade, (1, channels // 128)) + product
+    def attend(zb, k):
+        block = kv[zb, k].reshape(cores * chunk, channels)
+        for start in range(0, rows, BAND):
+            band = slice(start, start + BAND)
+            scores = lax.dot_general(
+                queries[band], block, NT, preferred_element_type=jnp.float32
+            )
+            scores = scores + jnp.tile(bias[band], (1, cores * chunk // 128))
+            newest = jnp.maximum(maxima[band], jnp.max(scores, axis=1, keepdims=True))
+            fade = jnp.exp2(maxima[band] - newest)
+            maxima[band] = newest
+            expo = jnp.exp2(scores - jnp.tile(newest, (1, cores * chunk // 128)))
+            summed = total[band] * fade
+            for j in range(cores * chunk // 128):
+                summed = summed + expo[:, j * 128 : (j + 1) * 128]
+            total[band] = summed
+            product = jnp.dot(
+                expo.astype(jnp.bfloat16), block, preferred_element_type=jnp.float32
+            )
+            acc[band] = acc[band] * jnp.tile(fade, (1, channels // 128)) + product
 
     def relay(t):
         d = t // chunks
@@ -213,7 +226,7 @@
 
             @pl.when(inside)
             def _(way=way, zb=zb):
-                arrival(zb * 2 + c, k).wait_recv()
+                arrival(zb, k, c).wait_recv()
 
                 @pl.when((z < deep - 1) if way == 0 else (z > 0))
                 def _():
@@ -225,40 +238,32 @@
 
     @pl.loop(0, deep * chunks)
     def _(t):
-        relay(t + ahead)
+        with jax.named_scope("relay"):
+            relay(t + ahead)
         d = t // chunks
         k = t % chunks
 
-        @pl.loop(0, 4)
-        def _(j):
-            side = j % 2
-            other = j // 2
+        @pl.loop(0, 2)
+        def _(side):
             zb = z + d * (2 * side - 1)
             inside = jnp.logical_and(zb >= 0, zb < deep)
 
             @pl.when(jnp.logical_and(inside, jnp.logical_or(side == 0, d > 0)))
             def _():
-                b = zb * 2 + c + other * (1 - 2 * c)
-
-                @pl.when(other == 1)
-                def _():
-                    arrival(b, k).wait_recv()
-
-                attend(b, k)
-
-    for weight in weights[2:4]:
-        weight.wait()
-    denominator = jnp.sum(total[...], axis=1, keepdims=True)
-    average = (acc[...] / denominator - centre) * gain + attn_shift[...]
-    attended = jnp.dot(
-        average.astype(jnp.bfloat16), wv[...], preferred_element_type=jnp.float32
-    ).astype(jnp.bfloat16)
-    field = (
-        kv[r].reshape(rows, channels).astype(jnp.float32)
-        + jnp.dot(attended, wo[...], preferred_element_type=jnp.float32)
-    ).astype(jnp.bfloat16)
-    hidden[...] = field
-    share_moments(1, field.astype(jnp.float32))
+                with jax.named_scope("wait"):
+                    arrival(zb, k, 1 - c).wait_recv()
+                with jax.named_scope("attend"):
+                    attend(zb, k)
+
+    with jax.named_scope("post"):
+        denominator = jnp.sum(total[...], axis=1, keepdims=True)
+        average = (acc[...] / denominator - centre) * gain + attn_shift[...]
+        field = (
+            own_rows().astype(jnp.float32)
+            + jnp.dot(average.astype(jnp.bfloat16), wv[...], preferred_element_type=jnp.float32)
+        ).astype(jnp.bfloat16)
+        hidden[...] = field
+        share_moments(1, field.astype(jnp.float32))
 
     up = pltpu.make_async_remote_copy(
         src_ref=hidden.at[pl.ds(0, wide)],
@@ -302,7 +307,8 @@
 
     for weight in weights[4:]:
         weight.wait()
-    centre, scale = gather_moments(1)
+    with jax.named_scope("stat1"):
+        centre, scale = gather_moments(1)
     gain = scale * conv_gain[...]
 
     def activate(values):
@@ -315,7 +321,8 @@
             if 0 <= y < lines:
                 stacked[y * wide : (y + 1) * wide, dy * channels : (dy + 1) * channels] = values
 
-    for line in range(lines):
+    with jax.named_scope("act"):
+      for line in range(lines):
         place(line, activate(hidden[line * wide : (line + 1) * wide]))
 
     @pl.when(r > 0)
@@ -339,9 +346,9 @@
         place(lines, jnp.zeros((wide, channels), jnp.bfloat16))
 
     half = 256
-    stores = []
     column = lax.broadcasted_iota(jnp.int32, (rows, half), 0) % wide
-    for start in range(0, channels, half):
+    with jax.named_scope("conv"):
+      for start in range(0, channels, half):
         cut = slice(start, start + half)
 
         def taps(dx):
@@ -353,15 +360,7 @@
             column < wide - 1, pltpu.roll(taps(2), rows - 1, 0), 0.0
         )
         encoded = hidden[:, cut].astype(jnp.float32) + (convolved + conv_bias[:, cut])
-        result[:, cut] = encoded.astype(jnp.bfloat16)
-        store = pltpu.make_async_copy(
-            result.at[:, cut], out.at[:, cut], store_sem.at[start // half]
-        )
-        store.start()
-        stores.append(store)
-
-    for store in stores:
-        store.wait()
+        out[:, cut] = encoded.astype(jnp.bfloat16)
 
 
 def local(n, latent, attn_gain, attn_shift, w_query, w_key, w_value, w_out,
@@ -376,11 +375,11 @@
     dma = pltpu.SemaphoreType.DMA
     encoded = pl.pallas_call(
         functools.partial(kernel, n, wide),
-        out_shape=jax.ShapeDtypeStruct((rows, channels), bf16),
+        out_shape=pltpu.VMEM((rows, channels), bf16),
         in_specs=[anywhere] * 6 + [vmem] * 5,
-        out_specs=anywhere,
+        out_specs=vmem,
         scratch_shapes=[
-            pltpu.VMEM((n, chunks, CHUNK, channels), bf16),
+            pltpu.VMEM((n // 2, chunks, 2, CHUNK, channels), bf16),
             square, square, square, square,
             pltpu.VMEM((3, 3 * channels, channels), bf16),
             square,
@@ -396,13 +395,11 @@
             dma((chunks,)),
             dma((13,)),
             dma((3, n // 2, chunks)),
-            dma((n, chunks)),
+            dma((n // 2, chunks, 2)),
             dma((2, n)),
             dma((2, n)),
             dma((2,)),
             dma((2,)),
-            pltpu.VMEM((rows, channels), bf16),
-            dma((channels // 256,)),
         ],
         compiler_params=pltpu.CompilerParams(
             collective_id=0, has_side_effects=True, vmem_limit_bytes=56 * 1024 * 1024

time: 56 us -> 53.5 us (0.955)
  Pallas kernels: 53.9 us -> 52.5 us
  local copies, waits for them, and re-layouts: 1.87 us -> 0.8 us
    pallas_call x1, Pallas kernels: 53.9 us -> 52.5 us  [local(): pl.pallas_call(functools.partial(kernel, n, wide), out_shape=pltpu.VMEM((...]
    unnamed x1, local copies, waits for them, and re-layouts: 1.87 us -> 0.8 us
where the time goes in v1:
time: 53.5 us; the launch traced here: 53.3 us
  Pallas kernels  52.5 us (98%)
  local copies, waits for them, and re-layouts  0.8 us (1%)
    pallas_call x1, Pallas kernels, local(): pl.pallas_call(functools.partial(kernel, n, wide), out_shape=pltpu.VMEM((...  52.5 us

profile of v1, /device:TPU:0, one launch (start us, length us, event | category | flops | bytes accessed | tf_op | source)
XLA Modules:
  0.0 53.3 jit_solution(17267398486772090407)
XLA Ops:
  0.0 52.5 %shard_map.109 = bf16[512,512]{1,0:T(8,128)(2,1)S(1)} custom-call(bf16[4,128,512]{2,1,0:T(8,128)(2,1)} %latent.1, bf16[512,512]{1,0:T(8,128)(2,1)} %w_query.1, bf16[512,512]{1,0:T(8,128)(2,1)} %w_key.1, bf16[512,512]{1,0:T(8,128)(2,1)} %w_value.1, bf16[512,512]{1,0:T(8,128)(2,1)} %w_out.1, bf16[3,3,512,512]{3,2,1,0:T(8,128)(2,1)} %w_conv.1, ...), custom_call_target="tpu_custom_call" | custom-call | tf_op jit(solution)/shard_map/pallas_call | solution.py:376
  52.5 0.8 %copy.13 = bf16[4,128,512]{2,1,0:T(8,128)(2,1)} copy(bf16[4,128,512]{2,1,0:T(8,128)(2,1)S(1)} %bitcast.6) | data formatting | bytes 1048576

commit v2 on v1

--- a/solution.py
+++ b/solution.py
@@ -11,7 +11,7 @@
 GROUPS = 32
 EPS = 1e-06
 CHUNK = 128
-BAND = 256
+BAND = 512
 MESH = pl.DeviceIdType.MESH
 LOG2E = math.log2(math.e)
 NT = (((1,), (1,)), ((), ()))
@@ -31,10 +31,11 @@
 def kernel(
     n, wide,
     latent, w_query, w_key, w_value, w_out, w_conv,
-    attn_gain, attn_shift, conv_gain, conv_shift, conv_bias,
+    gain_in, shift_in, conv_gain_in, conv_shift_in, bias_in,
     out,
-    kv, wq, wk, wv, wo, wc, ones, moments, queries, bias, maxima, total, acc, hidden, halo, stacked,
+    vector, kv, square, wc, ones, moments, queries, bias, maxima, total, acc, hidden, halo, stacked,
     load_sem, weight_sem, send_sem, recv_sem, stat_send, stat_recv, halo_send, halo_recv,
+    vector_sem, present,
 ):
     chunks, cores, chunk, channels = kv.shape[1:]
     rows = chunks * chunk
@@ -47,39 +48,44 @@
     c = r % 2
     partner = r + 1 - 2 * c
 
-    loads = [
-        pltpu.make_async_copy(latent.at[k], kv.at[z, k, c], load_sem.at[k]) for k in range(chunks)
+    load = pltpu.make_async_copy(latent, kv.at[z, :, c], load_sem)
+    load.start()
+
+    barrier = pltpu.get_barrier_semaphore()
+
+    def neighbours(act):
+        @pl.when(z < deep - 1)
+        def _():
+            act(r + 2)
+
+        @pl.when(z > 0)
+        def _():
+            act(r - 2)
+
+        act(partner)
+
+    def signal(semaphore, target):
+        pl.semaphore_signal(semaphore, inc=1, device_id=(img, target), device_id_type=MESH)
+
+    neighbours(functools.partial(signal, barrier))
+    vectors = [
+        pltpu.make_async_copy(source, vector.at[i], vector_sem)
+        for i, source in enumerate((gain_in, shift_in, conv_gain_in, conv_shift_in, bias_in))
     ]
-    for load in loads:
-        load.start()
+    attn_gain, attn_shift, conv_gain, conv_shift, conv_bias = (vector.at[i] for i in range(5))
+    wq, wk, wv, wo = (square.at[i] for i in range(4))
     weights = [
-        pltpu.make_async_copy(source, target, weight_sem.at[i])
-        for i, (source, target) in enumerate([(w_query, wq), (w_key, wk), (w_value, wv), (w_out, wo)])
+        pltpu.make_async_copy(source, square.at[i], weight_sem.at[0])
+        for i, source in enumerate((w_query, w_key, w_value, w_out))
     ]
-    weights += [
-        pltpu.make_async_copy(
-            w_conv.at[dy, dx],
-            wc.at[dx, pl.ds(dy * channels, channels)],
-            weight_sem.at[4 + dy * 3 + dx],
-        )
-        for dy in range(3)
-        for dx in range(3)
-    ]
-
-    barrier = pltpu.get_barrier_semaphore()
-
-    @pl.loop(1, n)
-    def _(j):
-        pl.semaphore_signal(
-            barrier, inc=1, device_id=(img, lax.rem(r + j, n)), device_id_type=MESH
-        )
+    taps_in = pltpu.make_async_copy(w_conv, wc, weight_sem.at[1])
 
     def piece(way, zb, k):
         target = (r + 2, r - 2, partner)[way]
         return pltpu.make_async_remote_copy(
             src_ref=kv.at[zb, k, c],
             dst_ref=kv.at[zb, k, c],
-            send_sem=send_sem.at[way, zb, k],
+            send_sem=send_sem.at[way],
             recv_sem=recv_sem.at[zb, k, c],
             device_id=(img, target),
             device_id_type=MESH,
@@ -89,7 +95,7 @@
         return pltpu.make_async_remote_copy(
             src_ref=kv.at[zb, k, core],
             dst_ref=kv.at[zb, k, core],
-            send_sem=send_sem.at[0, 0, 0],
+            send_sem=send_sem.at[0],
             recv_sem=recv_sem.at[zb, k, core],
             device_id=(img, partner),
             device_id_type=MESH,
@@ -99,18 +105,18 @@
         return pltpu.make_async_remote_copy(
             src_ref=moments.at[which, r],
             dst_ref=moments.at[which, r],
-            send_sem=stat_send.at[which, j],
-            recv_sem=stat_recv.at[which, r],
+            send_sem=stat_send.at[which],
+            recv_sem=stat_recv.at[which],
             device_id=(img, lax.rem(r + j, n)),
             device_id_type=MESH,
         )
 
-    def stat_arrival(which, b):
+    def stat_all(which):
         return pltpu.make_async_remote_copy(
-            src_ref=moments.at[which, b],
-            dst_ref=moments.at[which, b],
-            send_sem=stat_send.at[which, 0],
-            recv_sem=stat_recv.at[which, b],
+            src_ref=moments.at[which, pl.ds(0, n - 1)],
+            dst_ref=moments.at[which, pl.ds(0, n - 1)],
+            send_sem=stat_send.at[which],
+            recv_sem=stat_recv.at[which],
             device_id=(img, partner),
             device_id_type=MESH,
         )
@@ -129,26 +135,21 @@
 
         piece(2, z, k).start()
 
-    def share_moments(which, field):
+    def find_moments(which, field):
         mean = jnp.sum(field, axis=0, keepdims=True) * (1.0 / rows)
         offset = field - mean
         square = jnp.sum(offset * offset, axis=0, keepdims=True)
         moments[which, r, 0:1, :] = mean
         moments[which, r, 1:2, :] = square
 
+    def share_moments(which):
         @pl.loop(1, n)
         def _(j):
             stat_copy(which, j).start()
 
     def gather_moments(which):
-        @pl.loop(1, n)
-        def _(j):
-            stat_arrival(which, lax.rem(r + j, n)).wait_recv()
-
-        @pl.loop(1, n)
-        def _(j):
-            stat_copy(which, j).wait_send()
-
+        stat_all(which).wait_recv()
+        stat_all(which).wait_send()
         every = moments[which]
         means = every[:, 0, :]
         squares = every[:, 1, :]
@@ -161,17 +162,54 @@
         return centre, lax.rsqrt(variance + EPS)
 
     with jax.named_scope("load"):
-        for load in loads:
-            load.wait()
-    for weight in weights:
-        weight.start()
+        load.wait()
     with jax.named_scope("barrier"):
-        pl.semaphore_wait(barrier, n - 1)
+        pl.semaphore_wait(barrier, 1 + (z > 0).astype(jnp.int32) + (z < deep - 1).astype(jnp.int32))
+
+    early = chunks // 2
+
+    @pl.when(c == 0)
+    def _():
+        for k in range(early):
+            send_own(k)
+
+    for copy in vectors + weights + [taps_in]:
+        copy.start()
     with jax.named_scope("share0"):
-        send_own(0)
-        share_moments(0, own_rows().astype(jnp.float32))
-        for k in range(1, chunks):
+        find_moments(0, own_rows().astype(jnp.float32))
+
+    @pl.when(c == 1)
+    def _():
+        for k in range(early):
             send_own(k)
+
+    def chain(way):
+        first, last = (z == 0, z == deep - 1) if way == 0 else (z == deep - 1, z == 0)
+
+        @pl.when(jnp.logical_not(first))
+        def _():
+            pl.semaphore_wait(present.at[way], 1)
+
+        @pl.when(jnp.logical_not(last))
+        def _():
+            signal(present.at[way], r + 2 - 4 * way)
+
+    with jax.named_scope("present"):
+        @pl.when(z < deep // 2)
+        def _():
+            chain(0)
+            chain(1)
+
+        @pl.when(z >= deep // 2)
+        def _():
+            chain(1)
+            chain(0)
+
+        signal(present.at[2], partner)
+        pl.semaphore_wait(present.at[2], 1)
+    share_moments(0)
+    for k in range(early, chunks):
+        send_own(k)
 
     left_group = lax.broadcasted_iota(jnp.int32, (channels, channels), 0) // size
     right_group = lax.broadcasted_iota(jnp.int32, (channels, channels), 1) // size
@@ -180,8 +218,8 @@
     total[...] = jnp.zeros_like(total)
     acc[...] = jnp.zeros_like(acc)
 
-    for weight in weights[:4]:
-        weight.wait()
+    pltpu.make_async_copy(vector, vector, vector_sem).wait()
+    pltpu.make_async_copy(square, square, weight_sem.at[0]).wait()
     with jax.named_scope("fold"):
         wv[...] = jnp.dot(wv[...], wo[...], preferred_element_type=jnp.float32).astype(jnp.bfloat16)
     with jax.named_scope("stat0"):
@@ -263,7 +301,8 @@
             + jnp.dot(average.astype(jnp.bfloat16), wv[...], preferred_element_type=jnp.float32)
         ).astype(jnp.bfloat16)
         hidden[...] = field
-        share_moments(1, field.astype(jnp.float32))
+        find_moments(1, field.astype(jnp.float32))
+        share_moments(1)
 
     up = pltpu.make_async_remote_copy(
         src_ref=hidden.at[pl.ds(0, wide)],
@@ -290,23 +329,28 @@
     def _():
         down.start()
 
-    @pl.loop(0, deep * chunks)
-    def _(t):
-        zb = t // chunks
-        k = t % chunks
-
-        @pl.when(jnp.logical_and(z < deep - 1, zb <= z))
-        def _():
-            piece(0, zb, k).wait_send()
-
-        @pl.when(jnp.logical_and(z > 0, zb >= z))
-        def _():
-            piece(1, zb, k).wait_send()
-
-        piece(2, zb, k).wait_send()
-
-    for weight in weights[4:]:
-        weight.wait()
+    def sent(way, first, last):
+        part = kv.at[pl.ds(first, last - first), :, c]
+        pltpu.make_async_remote_copy(
+            src_ref=part,
+            dst_ref=part,
+            send_sem=send_sem.at[way],
+            recv_sem=recv_sem.at[0, 0, 0],
+            device_id=(img, partner),
+            device_id_type=MESH,
+        ).wait_send()
+
+    for here in range(deep):
+        @pl.when(z == here)
+        def _(here=here):
+            if here < deep - 1:
+                sent(0, 0, here + 1)
+            if here > 0:
+                sent(1, here, deep)
+
+    sent(2, 0, deep)
+
+    taps_in.wait()
     with jax.named_scope("stat1"):
         centre, scale = gather_moments(1)
     gain = scale * conv_gain[...]
@@ -352,7 +396,7 @@
         cut = slice(start, start + half)
 
         def taps(dx):
-            return jnp.dot(stacked[...], wc[dx, :, cut], preferred_element_type=jnp.float32)
+            return jnp.dot(stacked[...], wc[:, dx, :, cut].reshape(3 * channels, half), preferred_element_type=jnp.float32)
 
         convolved = taps(1)
         convolved = convolved + jnp.where(column > 0, pltpu.roll(taps(0), 1, 0), 0.0)
@@ -369,20 +413,19 @@
     rows = height * wide
     chunks = rows // CHUNK
     anywhere = pl.BlockSpec(memory_space=pl.ANY)
-    vmem = pl.BlockSpec(memory_space=pltpu.VMEM)
     bf16, f32 = jnp.bfloat16, jnp.float32
-    square = pltpu.VMEM((channels, channels), bf16)
     dma = pltpu.SemaphoreType.DMA
     encoded = pl.pallas_call(
         functools.partial(kernel, n, wide),
         out_shape=pltpu.VMEM((rows, channels), bf16),
-        in_specs=[anywhere] * 6 + [vmem] * 5,
-        out_specs=vmem,
+        in_specs=[anywhere] * 11,
+        out_specs=pl.BlockSpec(memory_space=pltpu.VMEM),
         scratch_shapes=[
+            pltpu.VMEM((5, 1, channels), f32),
             pltpu.VMEM((n // 2, chunks, 2, CHUNK, channels), bf16),
-            square, square, square, square,
-            pltpu.VMEM((3, 3 * channels, channels), bf16),
-            square,
+            pltpu.VMEM((4, channels, channels), bf16),
+            pltpu.VMEM((3, 3, channels, channels), bf16),
+            pltpu.VMEM((channels, channels), bf16),
             pltpu.VMEM((2, n, 2, channels), f32),
             pltpu.VMEM((rows, channels), bf16),
             pltpu.VMEM((rows, 128), f32),
@@ -392,14 +435,16 @@
             pltpu.VMEM((rows, channels), bf16),
             pltpu.VMEM((2, wide, channels), bf16),
             pltpu.VMEM((rows, 3 * channels), bf16),
-            dma((chunks,)),
-            dma((13,)),
-            dma((3, n // 2, chunks)),
+            dma,
+            dma((2,)),
+            dma((3,)),
             dma((n // 2, chunks, 2)),
-            dma((2, n)),
-            dma((2, n)),
             dma((2,)),
             dma((2,)),
+            dma((2,)),
+            dma((2,)),
+            dma,
+            pltpu.SemaphoreType.REGULAR((3,)),
         ],
         compiler_params=pltpu.CompilerParams(
             collective_id=0, has_side_effects=True, vmem_limit_bytes=56 * 1024 * 1024

time: 53.5 us -> 51.8 us (0.968)
  Pallas kernels: 52.5 us -> 50.8 us
    pallas_call x1, Pallas kernels: 52.5 us -> 50.8 us  [local(): pl.pallas_call(functools.partial(kernel, n, wide), out_shape=pltpu.VMEM((...]
where the time goes in v2:
time: 51.8 us; the launch traced here: 51.6 us
  Pallas kernels  50.8 us (98%)
  local copies, waits for them, and re-layouts  0.8 us (2%)
    pallas_call x1, Pallas kernels, local(): pl.pallas_call(functools.partial(kernel, n, wide), out_shape=pltpu.VMEM((...  50.8 us

profile of v2, /device:TPU:0, one launch (start us, length us, event | category | flops | bytes accessed | tf_op | source)
XLA Modules:
  0.0 51.6 jit_solution(6137241090975487818)
XLA Ops:
  0.0 50.8 %shard_map.109 = bf16[512,512]{1,0:T(8,128)(2,1)S(1)} custom-call(bf16[4,128,512]{2,1,0:T(8,128)(2,1)} %latent.1, bf16[512,512]{1,0:T(8,128)(2,1)} %w_query.1, bf16[512,512]{1,0:T(8,128)(2,1)} %w_key.1, bf16[512,512]{1,0:T(8,128)(2,1)} %w_value.1, bf16[512,512]{1,0:T(8,128)(2,1)} %w_out.1, bf16[3,3,512,512]{3,2,1,0:T(8,128)(2,1)} %w_conv.1, ...), custom_call_target="tpu_custom_call" | custom-call | tf_op jit(solution)/shard_map/pallas_call | solution.py:418
  50.8 0.8 %copy.13 = bf16[4,128,512]{2,1,0:T(8,128)(2,1)} copy(bf16[4,128,512]{2,1,0:T(8,128)(2,1)S(1)} %bitcast.6) | data formatting | bytes 1048576

commit v3 on v2

--- a/solution.py
+++ b/solution.py
@@ -11,7 +11,10 @@
 GROUPS = 32
 EPS = 1e-06
 CHUNK = 128
-BAND = 512
+UNIT = 2
+GROUP = 4
+DETOUR = 2
+PIECE = 64
 MESH = pl.DeviceIdType.MESH
 LOG2E = math.log2(math.e)
 NT = (((1,), (1,)), ((), ()))
@@ -29,13 +32,14 @@
 
 
 def kernel(
-    n, wide,
+    n, relief, wide,
     latent, w_query, w_key, w_value, w_out, w_conv,
     gain_in, shift_in, conv_gain_in, conv_shift_in, bias_in,
     out,
     vector, kv, square, wc, ones, moments, queries, bias, maxima, total, acc, hidden, halo, stacked,
     load_sem, weight_sem, send_sem, recv_sem, stat_send, stat_recv, halo_send, halo_recv,
     vector_sem, present,
+    detour, detour_recv, outgoing, answer, answer_recv, relayed, relayed_recv,
 ):
     chunks, cores, chunk, channels = kv.shape[1:]
     rows = chunks * chunk
@@ -47,6 +51,32 @@
     z = r // 2
     c = r % 2
     partner = r + 1 - 2 * c
+    both = jnp.logical_and
+    no = jnp.logical_not
+    units = chunks // UNIT
+    early = chunks // 2
+
+    member = img % GROUP
+    chief = img - member + GROUP - 1
+    is_chief = both(relief, member == GROUP - 1)
+    is_member = both(relief, member < GROUP - 1)
+    lower, upper = z == 1, z == deep - 2
+    inner = jnp.logical_or(lower, upper)
+    outer = jnp.logical_or(z == 0, z == deep - 1)
+    double = both(is_chief, inner)
+    idle = both(is_chief, outer)
+    helper = both(is_member, inner)
+    late = both(is_member, outer)
+    outward = 1 - 2 * lower.astype(jnp.int32)
+    inward = 1 - 2 * (z > 0).astype(jnp.int32)
+    way_out = lower.astype(jnp.int32)
+    direct = chunks - DETOUR
+    pieces = rows // PIECE
+    routes = [
+        GROUP - 1 if p < pieces // 2 else GROUP - 2 - p % 2 for p in range(pieces)
+    ]
+    legs = [p for p in range(pieces) if routes[p] == GROUP - 2]
+    slots = len(legs)
 
     load = pltpu.make_async_copy(latent, kv.at[z, :, c], load_sem)
     load.start()
@@ -64,10 +94,18 @@
 
         act(partner)
 
-    def signal(semaphore, target):
-        pl.semaphore_signal(semaphore, inc=1, device_id=(img, target), device_id_type=MESH)
+    def signal(semaphore, target, image=img):
+        pl.semaphore_signal(semaphore, inc=1, device_id=(image, target), device_id_type=MESH)
 
     neighbours(functools.partial(signal, barrier))
+    expected = 1 + (z > 0).astype(jnp.int32) + (z < deep - 1).astype(jnp.int32)
+    if relief:
+        for i in range(GROUP - 1):
+            @pl.when(double)
+            def _(i=i):
+                signal(barrier, r, chief - GROUP + 1 + i)
+
+        expected = expected + helper.astype(jnp.int32)
     vectors = [
         pltpu.make_async_copy(source, vector.at[i], vector_sem)
         for i, source in enumerate((gain_in, shift_in, conv_gain_in, conv_shift_in, bias_in))
@@ -124,16 +162,56 @@
     def own_rows():
         return kv[z, :, c].reshape(rows, channels)
 
+    def hop(source, target, send, recv, image, row):
+        return pltpu.make_async_remote_copy(
+            src_ref=source,
+            dst_ref=target,
+            send_sem=send,
+            recv_sem=recv,
+            device_id=(image, row),
+            device_id_type=MESH,
+        )
+
+    def detour_in(i, k):
+        return hop(
+            kv.at[z, k, c], detour.at[i, k - direct], send_sem.at[way_out],
+            detour_recv.at[i, k - direct], chief, r,
+        )
+
+    def detour_out(i, k):
+        return hop(
+            detour.at[i, k - direct], kv.at[z, k, c], send_sem.at[way_out],
+            recv_sem.at[z, k, c], chief - GROUP + 1 + i, r + 2 * outward,
+        )
+
+    def forward_detours(which):
+        for i, k in which:
+            detour_in(i, k).wait_recv()
+            detour_out(i, k).start()
+
+    far = [(i, k) for k in range(direct, chunks) for i in reversed(range(GROUP - 2))]
+
+    def open_way(way, k=0):
+        edge, gate = (z < deep - 1, upper) if way == 0 else (z > 0, lower)
+        shut = jnp.logical_or(is_chief, both(is_member, k >= direct))
+        return both(edge, no(both(gate, shut)))
+
     def send_own(k):
-        @pl.when(z < deep - 1)
-        def _():
-            piece(0, z, k).start()
-
-        @pl.when(z > 0)
-        def _():
-            piece(1, z, k).start()
-
-        piece(2, z, k).start()
+        for way in range(2):
+            @pl.when(open_way(way, k))
+            def _(way=way):
+                piece(way, z, k).start()
+
+        @pl.when(no(idle))
+        def _():
+            piece(2, z, k).start()
+
+    def send_detours():
+        if relief:
+            @pl.when(helper)
+            def _():
+                for k in range(direct, chunks):
+                    detour_in(member, k).start()
 
     def find_moments(which, field):
         mean = jnp.sum(field, axis=0, keepdims=True) * (1.0 / rows)
@@ -164,14 +242,13 @@
     with jax.named_scope("load"):
         load.wait()
     with jax.named_scope("barrier"):
-        pl.semaphore_wait(barrier, 1 + (z > 0).astype(jnp.int32) + (z < deep - 1).astype(jnp.int32))
-
-    early = chunks // 2
+        pl.semaphore_wait(barrier, expected)
 
     @pl.when(c == 0)
     def _():
         for k in range(early):
             send_own(k)
+        send_detours()
 
     for copy in vectors + weights + [taps_in]:
         copy.start()
@@ -182,6 +259,7 @@
     def _():
         for k in range(early):
             send_own(k)
+        send_detours()
 
     def chain(way):
         first, last = (z == 0, z == deep - 1) if way == 0 else (z == deep - 1, z == 0)
@@ -222,83 +300,182 @@
     pltpu.make_async_copy(square, square, weight_sem.at[0]).wait()
     with jax.named_scope("fold"):
         wv[...] = jnp.dot(wv[...], wo[...], preferred_element_type=jnp.float32).astype(jnp.bfloat16)
+    def relay(s):
+        d = s // chunks + 1
+        k = s % chunks
+        for way, zb in ((0, z - d), (1, z + d)):
+            @pl.when(both(no(idle), both(zb >= 0, zb < deep)))
+            def _(way=way, zb=zb):
+                arrival(zb, k, c).wait_recv()
+
+                @pl.when(open_way(way))
+                def _():
+                    piece(way, zb, k).start()
+
+                piece(2, zb, k).start()
+
+    with jax.named_scope("early"):
+        for s in range(early):
+            relay(s)
+            if relief and s == 0:
+                @pl.when(double)
+                def _():
+                    forward_detours([(GROUP - 2, k) for k in range(direct, chunks)])
+
+        if relief:
+            @pl.when(double)
+            def _():
+                forward_detours(far[: len(far) // 2])
+
     with jax.named_scope("stat0"):
         centre, scale = gather_moments(0)
     gain = scale * attn_gain[...]
-    positions = own_rows().astype(jnp.float32)
-    normed = ((positions - centre) * gain + attn_shift[...]).astype(jnp.bfloat16)
-    query = jnp.dot(normed, wq[...], preferred_element_type=jnp.float32).astype(jnp.bfloat16)
-    folded = lax.dot_general(query, wk[...], NT, preferred_element_type=jnp.float32) * (
-        LOG2E / math.sqrt(channels)
-    )
-    queries[...] = (folded * gain).astype(jnp.bfloat16)
-    constant = jnp.sum(folded * (attn_shift[...] - centre * gain), axis=1, keepdims=True)
-    bias[...] = jnp.broadcast_to(constant, bias.shape)
-
-    def attend(zb, k):
-        block = kv[zb, k].reshape(cores * chunk, channels)
-        for start in range(0, rows, BAND):
-            band = slice(start, start + BAND)
-            scores = lax.dot_general(
-                queries[band], block, NT, preferred_element_type=jnp.float32
-            )
-            scores = scores + jnp.tile(bias[band], (1, cores * chunk // 128))
-            newest = jnp.maximum(maxima[band], jnp.max(scores, axis=1, keepdims=True))
-            fade = jnp.exp2(maxima[band] - newest)
-            maxima[band] = newest
-            expo = jnp.exp2(scores - jnp.tile(newest, (1, cores * chunk // 128)))
-            summed = total[band] * fade
-            for j in range(cores * chunk // 128):
-                summed = summed + expo[:, j * 128 : (j + 1) * 128]
-            total[band] = summed
-            product = jnp.dot(
-                expo.astype(jnp.bfloat16), block, preferred_element_type=jnp.float32
-            )
-            acc[band] = acc[band] * jnp.tile(fade, (1, channels // 128)) + product
-
-    def relay(t):
-        d = t // chunks
-        k = t % chunks
-        for way, zb in ((0, z - d), (1, z + d)):
-            inside = jnp.logical_and(d > 0, jnp.logical_and(zb >= 0, zb < deep))
-
-            @pl.when(inside)
-            def _(way=way, zb=zb):
-                arrival(zb, k, c).wait_recv()
-
-                @pl.when((z < deep - 1) if way == 0 else (z > 0))
-                def _():
-                    piece(way, zb, k).start()
-
-                piece(2, zb, k).start()
-
-    ahead = jnp.where(jnp.logical_and(z > 0, z < deep - 1), chunks, 0)
-
-    @pl.loop(0, deep * chunks)
-    def _(t):
+
+    def project(positions, first):
+        band = slice(first, first + rows)
+        normed = ((positions - centre) * gain + attn_shift[...]).astype(jnp.bfloat16)
+        query = jnp.dot(normed, wq[...], preferred_element_type=jnp.float32).astype(jnp.bfloat16)
+        folded = lax.dot_general(query, wk[...], NT, preferred_element_type=jnp.float32) * (
+            LOG2E / math.sqrt(channels)
+        )
+        queries[band] = (folded * gain).astype(jnp.bfloat16)
+        constant = jnp.sum(folded * (attn_shift[...] - centre * gain), axis=1, keepdims=True)
+        bias[band] = jnp.broadcast_to(constant, (rows, 128))
+
+    with jax.named_scope("qproj"):
+        project(own_rows().astype(jnp.float32), 0)
+    if relief:
+        @pl.when(double)
+        def _():
+            with jax.named_scope("second"):
+                forward_detours(far[len(far) // 2 :])
+                for s in range(early, chunks):
+                    relay(s)
+                project(kv[z + outward, :, c].reshape(rows, channels).astype(jnp.float32), rows)
+
+    def attend(zb, h, first, count):
+        keys = UNIT * cores * chunk
+        band = slice(first, first + count)
+        block = kv[zb, pl.ds(UNIT * h, UNIT)].reshape(keys, channels)
+        scores = lax.dot_general(queries[band], block, NT, preferred_element_type=jnp.float32)
+        scores = scores + jnp.tile(bias[band], (1, keys // 128))
+        newest = jnp.maximum(maxima[band], jnp.max(scores, axis=1, keepdims=True))
+        fade = jnp.exp2(maxima[band] - newest)
+        maxima[band] = newest
+        expo = jnp.exp2(scores - jnp.tile(newest, (1, keys // 128)))
+        summed = total[band] * fade
+        for j in range(keys // 128):
+            summed = summed + expo[:, j * 128 : (j + 1) * 128]
+        total[band] = summed
+        product = jnp.dot(expo.astype(jnp.bfloat16), block, preferred_element_type=jnp.float32)
+        acc[band] = acc[band] * jnp.tile(fade, (1, channels // 128)) + product
+
+    def settle(zb, h):
+        with jax.named_scope("wait"):
+            for k in range(UNIT):
+                arrival(zb, UNIT * h + k, 1 - c).wait_recv()
+
+    def reach(u):
+        needed = (u // units - 1) * chunks + UNIT * (u % units + 1) - 1
+        return jnp.minimum(jnp.maximum(u + early, needed), (deep - 1) * chunks - 1)
+
+    def postponed(q, start, span, width):
+        inside = both(late, both(q >= start, q < start + span + width))
+        moved = jnp.where(q < start + span, q + width, q - span)
+        return jnp.where(inside, moved, q)
+
+    done = early + (chunks - early) * double.astype(jnp.int32)
+
+    @pl.loop(0, deep * units)
+    def _(u):
         with jax.named_scope("relay"):
-            relay(t + ahead)
-        d = t // chunks
-        k = t % chunks
+            @pl.loop(jnp.maximum(reach(u - 1) + 1, done), jnp.maximum(reach(u) + 1, done))
+            def _(q):
+                relay(postponed(q, chunks - DETOUR, chunks, DETOUR))
+
+        v = postponed(u, 2 * units - 1, units, 1)
+        d = v // units
+        h = v % units
+        final = both(double, u == (deep - 1) * units - 1)
 
         @pl.loop(0, 2)
         def _(side):
             zb = z + d * (2 * side - 1)
-            inside = jnp.logical_and(zb >= 0, zb < deep)
-
-            @pl.when(jnp.logical_and(inside, jnp.logical_or(side == 0, d > 0)))
+            inside = both(no(idle), both(zb >= 0, zb < deep))
+
+            @pl.when(both(both(inside, no(final)), jnp.logical_or(side == 0, d > 0)))
             def _():
-                with jax.named_scope("wait"):
-                    arrival(zb, k, 1 - c).wait_recv()
+                settle(zb, h)
                 with jax.named_scope("attend"):
-                    attend(zb, k)
+                    if relief:
+                        @pl.when(double)
+                        def _():
+                            attend(zb, h, 0, 2 * rows)
+
+                    @pl.when(no(double))
+                    def _():
+                        attend(zb, h, 0, rows)
+
+    def finish(first):
+        band = slice(first, first + rows)
+        denominator = jnp.sum(total[band], axis=1, keepdims=True)
+        average = (acc[band] / denominator - centre) * gain + attn_shift[...]
+        return average.astype(jnp.bfloat16)
+
+    def slab(ref, p):
+        return ref.at[pl.ds(p * PIECE, PIECE)]
+
+    def answer_direct(p):
+        return hop(
+            slab(outgoing, p), slab(answer, p), send_sem.at[3], answer_recv, chief,
+            r + 2 * outward,
+        )
+
+    def answer_in(p, slot):
+        return hop(
+            slab(outgoing, p), relayed.at[slot], send_sem.at[3], relayed_recv.at[slot],
+            chief - GROUP + 1 + routes[p], r,
+        )
+
+    def answer_out(p, slot):
+        return hop(
+            relayed.at[slot], slab(answer, p), send_sem.at[3], answer_recv, chief,
+            r + 2 * outward,
+        )
+
+    def leg(route):
+        return enumerate(p for p in range(pieces) if routes[p] == route)
+
+    if relief:
+        @pl.when(double)
+        def _():
+            remote = (deep - 1) * lower.astype(jnp.int32)
+            settle(remote, units - 1)
+            with jax.named_scope("answer"):
+                attend(remote, units - 1, rows, rows)
+                outgoing[...] = finish(rows)
+                for slot in range(slots):
+                    for route in (GROUP - 3, GROUP - 2):
+                        for other, p in leg(route):
+                            if other == slot:
+                                answer_in(p, slot).start()
+                for _, p in leg(GROUP - 1):
+                    answer_direct(p).start()
+                attend(remote, units - 1, 0, rows)
+
+        @pl.when(idle)
+        def _():
+            with jax.named_scope("answered"):
+                hop(outgoing, answer, send_sem.at[3], answer_recv, chief, r).wait_recv()
+
+    @pl.when(no(idle))
+    def _():
+        answer[...] = finish(0)
 
     with jax.named_scope("post"):
-        denominator = jnp.sum(total[...], axis=1, keepdims=True)
-        average = (acc[...] / denominator - centre) * gain + attn_shift[...]
         field = (
             own_rows().astype(jnp.float32)
-            + jnp.dot(average.astype(jnp.bfloat16), wv[...], preferred_element_type=jnp.float32)
+            + jnp.dot(answer[...], wv[...], preferred_element_type=jnp.float32)
         ).astype(jnp.bfloat16)
         hidden[...] = field
         find_moments(1, field.astype(jnp.float32))
@@ -329,26 +506,39 @@
     def _():
         down.start()
 
+    if relief:
+        for route in (GROUP - 3, GROUP - 2):
+            @pl.when(both(helper, member == route))
+            def _(route=route):
+                with jax.named_scope("leg"):
+                    for slot, p in leg(route):
+                        answer_in(p, slot).wait_recv()
+                        answer_out(p, slot).start()
+                    hop(relayed, relayed, send_sem.at[3], answer_recv, chief, r).wait_send()
+
+        @pl.when(double)
+        def _():
+            hop(detour, detour, send_sem.at[way_out], answer_recv, chief, r).wait_send()
+            hop(outgoing, outgoing, send_sem.at[3], answer_recv, chief, r).wait_send()
+
     def sent(way, first, last):
         part = kv.at[pl.ds(first, last - first), :, c]
-        pltpu.make_async_remote_copy(
-            src_ref=part,
-            dst_ref=part,
-            send_sem=send_sem.at[way],
-            recv_sem=recv_sem.at[0, 0, 0],
-            device_id=(img, partner),
-            device_id_type=MESH,
-        ).wait_send()
+        hop(part, part, send_sem.at[way], answer_recv, img, partner).wait_send()
 
     for here in range(deep):
-        @pl.when(z == here)
-        def _(here=here):
-            if here < deep - 1:
+        if here < deep - 1:
+            @pl.when(both(z == here, no(both(is_chief, upper))))
+            def _(here=here):
                 sent(0, 0, here + 1)
-            if here > 0:
+
+        if here > 0:
+            @pl.when(both(z == here, no(both(is_chief, lower))))
+            def _(here=here):
                 sent(1, here, deep)
 
-    sent(2, 0, deep)
+    @pl.when(no(idle))
+    def _():
+        sent(2, 0, deep)
 
     taps_in.wait()
     with jax.named_scope("stat1"):
@@ -407,7 +597,7 @@
         out[:, cut] = encoded.astype(jnp.bfloat16)
 
 
-def local(n, latent, attn_gain, attn_shift, w_query, w_key, w_value, w_out,
+def local(n, relief, latent, attn_gain, attn_shift, w_query, w_key, w_value, w_out,
           conv_gain, conv_shift, w_conv, conv_bias):
     height, wide, channels = latent.shape
     rows = height * wide
@@ -416,7 +606,7 @@
     bf16, f32 = jnp.bfloat16, jnp.float32
     dma = pltpu.SemaphoreType.DMA
     encoded = pl.pallas_call(
-        functools.partial(kernel, n, wide),
+        functools.partial(kernel, n, relief, wide),
         out_shape=pltpu.VMEM((rows, channels), bf16),
         in_specs=[anywhere] * 11,
         out_specs=pl.BlockSpec(memory_space=pltpu.VMEM),
@@ -427,17 +617,15 @@
             pltpu.VMEM((3, 3, channels, channels), bf16),
             pltpu.VMEM((channels, channels), bf16),
             pltpu.VMEM((2, n, 2, channels), f32),
-            pltpu.VMEM((rows, channels), bf16),
-            pltpu.VMEM((rows, 128), f32),
-            pltpu.VMEM((rows, 128), f32),
-            pltpu.VMEM((rows, 128), f32),
-            pltpu.VMEM((rows, channels), f32),
+            pltpu.VMEM((2 * rows, channels), bf16),
+            *[pltpu.VMEM((2 * rows, 128), f32)] * 3,
+            pltpu.VMEM((2 * rows, channels), f32),
             pltpu.VMEM((rows, channels), bf16),
             pltpu.VMEM((2, wide, channels), bf16),
             pltpu.VMEM((rows, 3 * channels), bf16),
             dma,
             dma((2,)),
-            dma((3,)),
+            dma((4,)),
             dma((n // 2, chunks, 2)),
             dma((2,)),
             dma((2,)),
@@ -445,6 +633,13 @@
             dma((2,)),
             dma,
             pltpu.SemaphoreType.REGULAR((3,)),
+            pltpu.VMEM((GROUP - 1, DETOUR, CHUNK, channels), bf16),
+            dma((GROUP - 1, DETOUR)),
+            pltpu.VMEM((rows, channels), bf16),
+            pltpu.VMEM((rows, channels), bf16),
+            dma,
+            pltpu.VMEM((rows // PIECE // 4, PIECE, channels), bf16),
+            dma((rows // PIECE // 4,)),
         ],
         compiler_params=pltpu.CompilerParams(
             collective_id=0, has_side_effects=True, vmem_limit_bytes=56 * 1024 * 1024
@@ -459,5 +654,7 @@
 def solution(mesh):
     in_specs = (P(("img", "row"), None, None), P(), P(), P(), P(), P(), P(), P(), P(), P(), P())
     out_specs = P(("img", "row"), None, None)
-    body = functools.partial(local, mesh.shape["row"])
+    images, n = mesh.shape["img"], mesh.shape["row"]
+    relief = images % GROUP == 0 and n // 2 >= GROUP
+    body = functools.partial(local, n, relief)
     return jax.shard_map(body, mesh=mesh, in_specs=in_specs, out_specs=out_specs, check_vma=False)

time: 51.8 us -> 48.5 us (0.936)
  the two profiles are of different devices: /device:TPU:0 before, /device:TPU:7 now
where the time goes in v3:
time: 48.5 us; the launch traced here: 48.3 us
  Pallas kernels  47.5 us (98%)
  local copies, waits for them, and re-layouts  0.8 us (2%)
    pallas_call x1, Pallas kernels, local(): pl.pallas_call(functools.partial(kernel, n, relief, wide), out_shape=pltp...  47.5 us

profile of v3, /device:TPU:7, one launch (start us, length us, event | category | flops | bytes accessed | tf_op | source)
XLA Modules:
  0.0 48.3 jit_solution(9287135681590004537)
XLA Ops:
  0.0 47.5 %shard_map.109 = bf16[512,512]{1,0:T(8,128)(2,1)S(1)} custom-call(bf16[4,128,512]{2,1,0:T(8,128)(2,1)} %latent.1, bf16[512,512]{1,0:T(8,128)(2,1)} %w_query.1, bf16[512,512]{1,0:T(8,128)(2,1)} %w_key.1, bf16[512,512]{1,0:T(8,128)(2,1)} %w_value.1, bf16[512,512]{1,0:T(8,128)(2,1)} %w_out.1, bf16[3,3,512,512]{3,2,1,0:T(8,128)(2,1)} %w_conv.1, ...), custom_call_target="tpu_custom_call" | custom-call | tf_op jit(solution)/shard_map/pallas_call | solution.py:608
  47.5 0.8 %copy.13 = bf16[4,128,512]{2,1,0:T(8,128)(2,1)} copy(bf16[4,128,512]{2,1,0:T(8,128)(2,1)S(1)} %bitcast.6) | data formatting | bytes 1048576

commit v4 on v3

--- a/solution.py
+++ b/solution.py
@@ -13,7 +13,11 @@
 CHUNK = 128
 UNIT = 2
 GROUP = 4
+CHIEF = 1
+NEAR = (0, 3)
+FAR = 2
 DETOUR = 2
+BRIDGE = 1
 PIECE = 64
 MESH = pl.DeviceIdType.MESH
 LOG2E = math.log2(math.e)
@@ -39,7 +43,7 @@
     vector, kv, square, wc, ones, moments, queries, bias, maxima, total, acc, hidden, halo, stacked,
     load_sem, weight_sem, send_sem, recv_sem, stat_send, stat_recv, halo_send, halo_recv,
     vector_sem, present,
-    detour, detour_recv, outgoing, answer, answer_recv, relayed, relayed_recv,
+    carried, carried_recv, detour, detour_recv, outgoing, answer, answer_recv, relayed, relayed_recv,
 ):
     chunks, cores, chunk, channels = kv.shape[1:]
     rows = chunks * chunk
@@ -57,9 +61,9 @@
     early = chunks // 2
 
     member = img % GROUP
-    chief = img - member + GROUP - 1
-    is_chief = both(relief, member == GROUP - 1)
-    is_member = both(relief, member < GROUP - 1)
+    chief = img - member + CHIEF
+    is_chief = both(relief, member == CHIEF)
+    is_member = both(relief, member != CHIEF)
     lower, upper = z == 1, z == deep - 2
     inner = jnp.logical_or(lower, upper)
     outer = jnp.logical_or(z == 0, z == deep - 1)
@@ -67,16 +71,15 @@
     idle = both(is_chief, outer)
     helper = both(is_member, inner)
     late = both(is_member, outer)
+    bridge = relief and deep == GROUP
+    porter = jnp.where(c == 0, NEAR[1], FAR)
+    carries = both(both(bridge, helper), member == porter)
     outward = 1 - 2 * lower.astype(jnp.int32)
     inward = 1 - 2 * (z > 0).astype(jnp.int32)
     way_out = lower.astype(jnp.int32)
     direct = chunks - DETOUR
     pieces = rows // PIECE
-    routes = [
-        GROUP - 1 if p < pieces // 2 else GROUP - 2 - p % 2 for p in range(pieces)
-    ]
-    legs = [p for p in range(pieces) if routes[p] == GROUP - 2]
-    slots = len(legs)
+    routes = [(NEAR[0], NEAR[1], CHIEF, CHIEF, NEAR[0], CHIEF, CHIEF, CHIEF)[p % 8] for p in range(pieces)]
 
     load = pltpu.make_async_copy(latent, kv.at[z, :, c], load_sem)
     load.start()
@@ -100,12 +103,16 @@
     neighbours(functools.partial(signal, barrier))
     expected = 1 + (z > 0).astype(jnp.int32) + (z < deep - 1).astype(jnp.int32)
     if relief:
-        for i in range(GROUP - 1):
+        for i in (*NEAR, FAR):
             @pl.when(double)
             def _(i=i):
-                signal(barrier, r, chief - GROUP + 1 + i)
-
-        expected = expected + helper.astype(jnp.int32)
+                signal(barrier, r, chief - CHIEF + i)
+
+        @pl.when(carries)
+        def _():
+            signal(barrier, r, chief)
+
+        expected = expected + helper.astype(jnp.int32) + both(bridge, double).astype(jnp.int32)
     vectors = [
         pltpu.make_async_copy(source, vector.at[i], vector_sem)
         for i, source in enumerate((gain_in, shift_in, conv_gain_in, conv_shift_in, bias_in))
@@ -181,7 +188,7 @@
     def detour_out(i, k):
         return hop(
             detour.at[i, k - direct], kv.at[z, k, c], send_sem.at[way_out],
-            recv_sem.at[z, k, c], chief - GROUP + 1 + i, r + 2 * outward,
+            recv_sem.at[z, k, c], chief - CHIEF + i, r + 2 * outward,
         )
 
     def forward_detours(which):
@@ -189,7 +196,21 @@
             detour_in(i, k).wait_recv()
             detour_out(i, k).start()
 
-    far = [(i, k) for k in range(direct, chunks) for i in reversed(range(GROUP - 2))]
+    later = [(i, k) for k in range(direct, chunks) for i in (NEAR[1], FAR)]
+
+    crossing = range(chunks - BRIDGE, chunks)
+
+    def bridge_in(j):
+        return hop(
+            kv.at[z, crossing[j], c], carried.at[j], send_sem.at[1 - way_out],
+            carried_recv.at[j], chief - CHIEF + porter, r,
+        )
+
+    def bridge_out(j):
+        return hop(
+            carried.at[j], kv.at[z, crossing[j], c], send_sem.at[4],
+            recv_sem.at[z, crossing[j], c], chief, r - 2 * outward,
+        )
 
     def open_way(way, k=0):
         edge, gate = (z < deep - 1, upper) if way == 0 else (z > 0, lower)
@@ -198,7 +219,9 @@
 
     def send_own(k):
         for way in range(2):
-            @pl.when(open_way(way, k))
+            bridged = both(both(bridge and k in crossing, double), way != way_out)
+
+            @pl.when(both(open_way(way, k), no(bridged)))
             def _(way=way):
                 piece(way, z, k).start()
 
@@ -208,6 +231,11 @@
 
     def send_detours():
         if relief:
+            @pl.when(both(bridge, double))
+            def _():
+                for j in range(BRIDGE):
+                    bridge_in(j).start()
+
             @pl.when(helper)
             def _():
                 for k in range(direct, chunks):
@@ -286,6 +314,13 @@
         signal(present.at[2], partner)
         pl.semaphore_wait(present.at[2], 1)
     share_moments(0)
+    if bridge:
+        @pl.when(carries)
+        def _():
+            for j in range(BRIDGE):
+                bridge_in(j).wait_recv()
+                bridge_out(j).start()
+
     for k in range(early, chunks):
         send_own(k)
 
@@ -320,12 +355,8 @@
             if relief and s == 0:
                 @pl.when(double)
                 def _():
-                    forward_detours([(GROUP - 2, k) for k in range(direct, chunks)])
-
-        if relief:
-            @pl.when(double)
-            def _():
-                forward_detours(far[: len(far) // 2])
+                    forward_detours([(NEAR[0], k) for k in range(direct, chunks)])
+
 
     with jax.named_scope("stat0"):
         centre, scale = gather_moments(0)
@@ -341,17 +372,6 @@
         queries[band] = (folded * gain).astype(jnp.bfloat16)
         constant = jnp.sum(folded * (attn_shift[...] - centre * gain), axis=1, keepdims=True)
         bias[band] = jnp.broadcast_to(constant, (rows, 128))
-
-    with jax.named_scope("qproj"):
-        project(own_rows().astype(jnp.float32), 0)
-    if relief:
-        @pl.when(double)
-        def _():
-            with jax.named_scope("second"):
-                forward_detours(far[len(far) // 2 :])
-                for s in range(early, chunks):
-                    relay(s)
-                project(kv[z + outward, :, c].reshape(rows, channels).astype(jnp.float32), rows)
 
     def attend(zb, h, first, count):
         keys = UNIT * cores * chunk
@@ -375,9 +395,26 @@
             for k in range(UNIT):
                 arrival(zb, UNIT * h + k, 1 - c).wait_recv()
 
+    with jax.named_scope("qproj"):
+        project(own_rows().astype(jnp.float32), 0)
+    if relief:
+        @pl.when(double)
+        def _():
+            with jax.named_scope("second"):
+                settle(z, 0)
+                attend(z, 0, 0, rows)
+                forward_detours(later[: len(later) // 2])
+                for h in range(1, units):
+                    settle(z, h)
+                    attend(z, h, 0, rows)
+                for s in range(early, chunks):
+                    relay(s)
+                project(kv[z + outward, :, c].reshape(rows, channels).astype(jnp.float32), rows)
+
     def reach(u):
         needed = (u // units - 1) * chunks + UNIT * (u % units + 1) - 1
-        return jnp.minimum(jnp.maximum(u + early, needed), (deep - 1) * chunks - 1)
+        lead = early + double.astype(jnp.int32)
+        return jnp.minimum(jnp.maximum(u + lead, needed), (deep - 1) * chunks - 1)
 
     def postponed(q, start, span, width):
         inside = both(late, both(q >= start, q < start + span + width))
@@ -386,38 +423,47 @@
 
     done = early + (chunks - early) * double.astype(jnp.int32)
 
-    @pl.loop(0, deep * units)
+    reached = jnp.maximum(z, deep - 1 - z) + 1
+    steps = jnp.where(idle, 0, units * reached - double.astype(jnp.int32))
+
+    @pl.loop(0, steps)
     def _(u):
         with jax.named_scope("relay"):
             @pl.loop(jnp.maximum(reach(u - 1) + 1, done), jnp.maximum(reach(u) + 1, done))
             def _(q):
-                relay(postponed(q, chunks - DETOUR, chunks, DETOUR))
-
-        v = postponed(u, 2 * units - 1, units, 1)
+                relay(postponed(q, chunks - DETOUR, chunks + UNIT, DETOUR))
+
+        if relief:
+            @pl.when(both(double, u == 1))
+            def _():
+                forward_detours(later[len(later) // 2 :])
+
+        v = postponed(u, 2 * units - 1, units + 1, 1)
         d = v // units
         h = v % units
-        final = both(double, u == (deep - 1) * units - 1)
-
         @pl.loop(0, 2)
         def _(side):
-            zb = z + d * (2 * side - 1)
-            inside = both(no(idle), both(zb >= 0, zb < deep))
-
-            @pl.when(both(both(inside, no(final)), jnp.logical_or(side == 0, d > 0)))
+            zb = z + d * (2 * side - 1) * (1 - 2 * upper.astype(jnp.int32))
+            inside = both(zb >= 0, zb < deep)
+
+            @pl.when(both(inside, jnp.logical_or(side == 0, d > 0)))
             def _():
-                settle(zb, h)
+                @pl.when(no(both(double, d == 0)))
+                def _():
+                    settle(zb, h)
+
                 with jax.named_scope("attend"):
                     if relief:
                         @pl.when(double)
                         def _():
-                            attend(zb, h, 0, 2 * rows)
+                            attend(zb, h, rows, rows)
 
                     @pl.when(no(double))
                     def _():
                         attend(zb, h, 0, rows)
 
-    def finish(first):
-        band = slice(first, first + rows)
+    def finish(first, count):
+        band = slice(first, first + count)
         denominator = jnp.sum(total[band], axis=1, keepdims=True)
         average = (acc[band] / denominator - centre) * gain + attn_shift[...]
         return average.astype(jnp.bfloat16)
@@ -434,7 +480,7 @@
     def answer_in(p, slot):
         return hop(
             slab(outgoing, p), relayed.at[slot], send_sem.at[3], relayed_recv.at[slot],
-            chief - GROUP + 1 + routes[p], r,
+            chief - CHIEF + routes[p], r,
         )
 
     def answer_out(p, slot):
@@ -443,8 +489,8 @@
             r + 2 * outward,
         )
 
-    def leg(route):
-        return enumerate(p for p in range(pieces) if routes[p] == route)
+    def legs_of(route):
+        return [p for p in range(pieces) if routes[p] == route]
 
     if relief:
         @pl.when(double)
@@ -452,16 +498,33 @@
             remote = (deep - 1) * lower.astype(jnp.int32)
             settle(remote, units - 1)
             with jax.named_scope("answer"):
-                attend(remote, units - 1, rows, rows)
-                outgoing[...] = finish(rows)
-                for slot in range(slots):
-                    for route in (GROUP - 3, GROUP - 2):
-                        for other, p in leg(route):
-                            if other == slot:
-                                answer_in(p, slot).start()
-                for _, p in leg(GROUP - 1):
-                    answer_direct(p).start()
-                attend(remote, units - 1, 0, rows)
+                for half in range(2):
+                    size = rows // 2
+                    attend(remote, units - 1, rows + half * size, size)
+                    outgoing[half * size : (half + 1) * size] = finish(rows + half * size, size)
+                    for p in range(half * pieces // 2, (half + 1) * pieces // 2):
+                        if routes[p] == CHIEF:
+                            answer_direct(p).start()
+                        else:
+                            answer_in(p, legs_of(routes[p]).index(p)).start()
+
+            @pl.loop(units, units * (deep - 1))
+            def _(u):
+                @pl.loop(0, 2)
+                def _(side):
+                    zb = z + u // units * (2 * side - 1)
+
+                    @pl.when(both(zb >= 0, zb < deep))
+                    def _():
+                        attend(zb, u % units, 0, rows)
+
+        for route in NEAR:
+            @pl.when(both(helper, member == route))
+            def _(route=route):
+                with jax.named_scope("leg"):
+                    for slot, p in enumerate(legs_of(route)):
+                        answer_in(p, slot).wait_recv()
+                        answer_out(p, slot).start()
 
         @pl.when(idle)
         def _():
@@ -470,7 +533,7 @@
 
     @pl.when(no(idle))
     def _():
-        answer[...] = finish(0)
+        answer[...] = finish(0, rows)
 
     with jax.named_scope("post"):
         field = (
@@ -507,19 +570,22 @@
         down.start()
 
     if relief:
-        for route in (GROUP - 3, GROUP - 2):
+        for route in NEAR:
             @pl.when(both(helper, member == route))
             def _(route=route):
-                with jax.named_scope("leg"):
-                    for slot, p in leg(route):
-                        answer_in(p, slot).wait_recv()
-                        answer_out(p, slot).start()
-                    hop(relayed, relayed, send_sem.at[3], answer_recv, chief, r).wait_send()
+                passed = relayed.at[pl.ds(0, len(legs_of(route)))]
+                hop(passed, passed, send_sem.at[3], answer_recv, chief, r).wait_send()
 
         @pl.when(double)
         def _():
-            hop(detour, detour, send_sem.at[way_out], answer_recv, chief, r).wait_send()
+            passed = detour.at[pl.ds(0, GROUP - 1)]
+            hop(passed, passed, send_sem.at[way_out], answer_recv, chief, r).wait_send()
             hop(outgoing, outgoing, send_sem.at[3], answer_recv, chief, r).wait_send()
+
+        if bridge:
+            @pl.when(carries)
+            def _():
+                hop(carried, carried, send_sem.at[4], answer_recv, chief, r).wait_send()
 
     def sent(way, first, last):
         part = kv.at[pl.ds(first, last - first), :, c]
@@ -625,7 +691,7 @@
             pltpu.VMEM((rows, 3 * channels), bf16),
             dma,
             dma((2,)),
-            dma((4,)),
+            dma((5,)),
             dma((n // 2, chunks, 2)),
             dma((2,)),
             dma((2,)),
@@ -633,8 +699,10 @@
             dma((2,)),
             dma,
             pltpu.SemaphoreType.REGULAR((3,)),
-            pltpu.VMEM((GROUP - 1, DETOUR, CHUNK, channels), bf16),
-            dma((GROUP - 1, DETOUR)),
+            pltpu.VMEM((BRIDGE, CHUNK, channels), bf16),
+            dma((BRIDGE,)),
+            pltpu.VMEM((GROUP, DETOUR, CHUNK, channels), bf16),
+            dma((GROUP, DETOUR)),
             pltpu.VMEM((rows, channels), bf16),
             pltpu.VMEM((rows, channels), bf16),
             dma,

time: 48.5 us -> 46.8 us (0.965)
  the two profiles are of different devices: /device:TPU:7 before, /device:TPU:0 now
where the time goes in v4:
time: 46.8 us; the launch traced here: 46.3 us
  Pallas kernels  45.5 us (97%)
  local copies, waits for them, and re-layouts  0.8 us (2%)
    pallas_call x1, Pallas kernels, local(): pl.pallas_call(functools.partial(kernel, n, relief, wide), out_shape=pltp...  45.5 us

profile of v4, /device:TPU:0, one launch (start us, length us, event | category | flops | bytes accessed | tf_op | source)
XLA Modules:
  0.0 46.3 jit_solution(17333315467187785530)
XLA Ops:
  0.0 45.5 %shard_map.109 = bf16[512,512]{1,0:T(8,128)(2,1)S(1)} custom-call(bf16[4,128,512]{2,1,0:T(8,128)(2,1)} %latent.1, bf16[512,512]{1,0:T(8,128)(2,1)} %w_query.1, bf16[512,512]{1,0:T(8,128)(2,1)} %w_key.1, bf16[512,512]{1,0:T(8,128)(2,1)} %w_value.1, bf16[512,512]{1,0:T(8,128)(2,1)} %w_out.1, bf16[3,3,512,512]{3,2,1,0:T(8,128)(2,1)} %w_conv.1, ...), custom_call_target="tpu_custom_call" | custom-call | tf_op jit(solution)/shard_map/pallas_call | solution.py:674
  45.5 0.8 %copy.13 = bf16[4,128,512]{2,1,0:T(8,128)(2,1)} copy(bf16[4,128,512]{2,1,0:T(8,128)(2,1)S(1)} %bitcast.6) | data formatting | bytes 1048576

commit v5 on v4

--- a/solution.py
+++ b/solution.py
@@ -18,7 +18,8 @@
 FAR = 2
 DETOUR = 2
 BRIDGE = 1
-PIECE = 64
+LENT = 1
+PIECE = 32
 MESH = pl.DeviceIdType.MESH
 LOG2E = math.log2(math.e)
 NT = (((1,), (1,)), ((), ()))
@@ -29,10 +30,23 @@
     rest = row - high
     mid = rest.astype(jnp.bfloat16).astype(jnp.float32)
     low = rest - mid
-    index = lax.broadcasted_iota(jnp.int32, (16, row.shape[1]), 0)
-    parts = jnp.where(index == 0, high, jnp.where(index == 1, mid, jnp.where(index == 2, low, 0.0)))
+    lanes = ones.shape[0]
+    slices = row.shape[1] // lanes
+    depth = -(-3 * slices // 16) * 16
+    index = lax.broadcasted_iota(jnp.int32, (depth, lanes), 0)
+    parts = jnp.zeros((depth, lanes), jnp.float32)
+    for i in range(slices):
+        for j, part in enumerate((high, mid, low)):
+            piece = part[:, i * lanes : (i + 1) * lanes]
+            parts = jnp.where(index == 3 * i + j, piece, parts)
     sums = jnp.dot(parts.astype(jnp.bfloat16), ones, preferred_element_type=jnp.float32)
-    return jnp.sum(sums, axis=0, keepdims=True)
+    return jnp.concatenate(
+        [
+            jnp.sum(jnp.where(index // 3 == i, sums, 0.0), axis=0, keepdims=True)
+            for i in range(slices)
+        ],
+        axis=1,
+    )
 
 
 def kernel(
@@ -79,7 +93,7 @@
     way_out = lower.astype(jnp.int32)
     direct = chunks - DETOUR
     pieces = rows // PIECE
-    routes = [(NEAR[0], NEAR[1], CHIEF, CHIEF, NEAR[0], CHIEF, CHIEF, CHIEF)[p % 8] for p in range(pieces)]
+    routes = [(NEAR[0], NEAR[0], NEAR[1], NEAR[1], CHIEF, CHIEF, CHIEF, CHIEF, NEAR[0], NEAR[0], CHIEF, CHIEF, CHIEF, CHIEF, CHIEF, CHIEF)[p % 16] for p in range(pieces)]
 
     load = pltpu.make_async_copy(latent, kv.at[z, :, c], load_sem)
     load.start()
@@ -166,6 +180,13 @@
             device_id_type=MESH,
         )
 
+    def lent(way, zb):
+        target = (r + 2, r - 2, partner)[way]
+        return hop(
+            kv.at[zb, LENT, 0], kv.at[zb, LENT, 0], send_sem.at[5 + way],
+            recv_sem.at[zb, LENT, 0], img, target,
+        )
+
     def own_rows():
         return kv[z, :, c].reshape(rows, channels)
 
@@ -221,11 +242,18 @@
         for way in range(2):
             bridged = both(both(bridge and k in crossing, double), way != way_out)
 
-            @pl.when(both(open_way(way, k), no(bridged)))
+            mine = both(open_way(way, k), no(bridged))
+
+            @pl.when(both(mine, c == 1) if k == LENT else mine)
             def _(way=way):
                 piece(way, z, k).start()
 
-        @pl.when(no(idle))
+        if k == LENT:
+            @pl.when(c == 0)
+            def _():
+                lent(2, z).start()
+
+        @pl.when(both(no(idle), no(both(c == 0, k == LENT))))
         def _():
             piece(2, z, k).start()
 
@@ -289,6 +317,14 @@
             send_own(k)
         send_detours()
 
+    @pl.when(c == 1)
+    def _():
+        lent(2, z).wait_recv()
+        for way in range(2):
+            @pl.when(open_way(way))
+            def _(way=way):
+                lent(way, z).start()
+
     def chain(way):
         first, last = (z == 0, z == deep - 1) if way == 0 else (z == deep - 1, z == 0)
 
@@ -324,8 +360,8 @@
     for k in range(early, chunks):
         send_own(k)
 
-    left_group = lax.broadcasted_iota(jnp.int32, (channels, channels), 0) // size
-    right_group = lax.broadcasted_iota(jnp.int32, (channels, channels), 1) // size
+    left_group = lax.broadcasted_iota(jnp.int32, ones.shape, 0) // size
+    right_group = lax.broadcasted_iota(jnp.int32, ones.shape, 1) // size
     ones[...] = jnp.where(left_group == right_group, 1.0, 0.0).astype(jnp.bfloat16)
     maxima[...] = jnp.full_like(maxima, -1e30)
     total[...] = jnp.zeros_like(total)
@@ -339,7 +375,9 @@
         d = s // chunks + 1
         k = s % chunks
         for way, zb in ((0, z - d), (1, z + d)):
-            @pl.when(both(no(idle), both(zb >= 0, zb < deep)))
+            inside = both(no(idle), both(zb >= 0, zb < deep))
+
+            @pl.when(both(inside, no(both(c == 0, k == LENT))))
             def _(way=way, zb=zb):
                 arrival(zb, k, c).wait_recv()
 
@@ -348,6 +386,16 @@
                     piece(way, zb, k).start()
 
                 piece(2, zb, k).start()
+
+            @pl.when(both(inside, both(c == 1, k == LENT)))
+            def _(way=way, zb=zb):
+                lent(way, zb).wait_recv()
+
+                @pl.when(open_way(way))
+                def _():
+                    lent(way, zb).start()
+
+                lent(2, zb).start()
 
     with jax.named_scope("early"):
         for s in range(early):
@@ -392,8 +440,18 @@
 
     def settle(zb, h):
         with jax.named_scope("wait"):
-            for k in range(UNIT):
-                arrival(zb, UNIT * h + k, 1 - c).wait_recv()
+            for i in range(UNIT):
+                k = UNIT * h + i
+
+                @pl.when(no(both(c == 1, k == LENT)))
+                def _(k=k):
+                    arrival(zb, k, 1 - c).wait_recv()
+
+                known = jnp.logical_or(zb == z, both(double, zb == z + outward))
+
+                @pl.when(both(both(c == 0, k == LENT), no(known)))
+                def _(k=k):
+                    arrival(zb, k, 0).wait_recv()
 
     with jax.named_scope("qproj"):
         project(own_rows().astype(jnp.float32), 0)
@@ -409,10 +467,16 @@
                     attend(z, h, 0, rows)
                 for s in range(early, chunks):
                     relay(s)
+                @pl.when(c == 0)
+                def _():
+                    arrival(z + outward, LENT, 0).wait_recv()
+
                 project(kv[z + outward, :, c].reshape(rows, channels).astype(jnp.float32), rows)
 
     def reach(u):
         needed = (u // units - 1) * chunks + UNIT * (u % units + 1) - 1
+        soon = both(late, u == 3 * units - 1).astype(jnp.int32)
+        needed = needed + UNIT * soon
         lead = early + double.astype(jnp.int32)
         return jnp.minimum(jnp.maximum(u + lead, needed), (deep - 1) * chunks - 1)
 
@@ -465,7 +529,7 @@
     def finish(first, count):
         band = slice(first, first + count)
         denominator = jnp.sum(total[band], axis=1, keepdims=True)
-        average = (acc[band] / denominator - centre) * gain + attn_shift[...]
+        average = (acc[band] * (1.0 / denominator) - centre) * gain + attn_shift[...]
         return average.astype(jnp.bfloat16)
 
     def slab(ref, p):
@@ -588,8 +652,19 @@
                 hop(carried, carried, send_sem.at[4], answer_recv, chief, r).wait_send()
 
     def sent(way, first, last):
-        part = kv.at[pl.ds(first, last - first), :, c]
-        hop(part, part, send_sem.at[way], answer_recv, img, partner).wait_send()
+        blocks = pl.ds(first, last - first)
+
+        def drained(part, semaphore):
+            hop(part, part, semaphore, answer_recv, img, partner).wait_send()
+
+        @pl.when(c == 0)
+        def _():
+            drained(kv.at[blocks, pl.ds(0, chunks - 1), 0], send_sem.at[way])
+
+        @pl.when(c == 1)
+        def _():
+            drained(kv.at[blocks, :, 1], send_sem.at[way])
+            drained(kv.at[blocks, LENT, 0], send_sem.at[5 + way])
 
     for here in range(deep):
         if here < deep - 1:
@@ -602,18 +677,31 @@
             def _(here=here):
                 sent(1, here, deep)
 
-    @pl.when(no(idle))
-    def _():
-        sent(2, 0, deep)
+    @pl.when(both(no(idle), c == 0))
+    def _():
+        part = kv.at[pl.ds(0, deep), pl.ds(0, chunks - 1), 0]
+        hop(part, part, send_sem.at[2], answer_recv, img, partner).wait_send()
+
+    @pl.when(c == 0)
+    def _():
+        lent(2, z).wait_send()
+
+    @pl.when(both(no(idle), c == 1))
+    def _():
+        part = kv.at[pl.ds(0, deep), :, 1]
+        hop(part, part, send_sem.at[2], answer_recv, img, partner).wait_send()
+        part = kv.at[pl.ds(0, deep - 1), LENT, 0]
+        hop(part, part, send_sem.at[7], answer_recv, img, partner).wait_send()
 
     taps_in.wait()
     with jax.named_scope("stat1"):
         centre, scale = gather_moments(1)
-    gain = scale * conv_gain[...]
+    half_gain = 0.5 * scale * conv_gain[...]
+    half_shift = 0.5 * conv_shift[...] - centre * half_gain
 
     def activate(values):
-        v = (values.astype(jnp.float32) - centre) * gain + conv_shift[...]
-        return (v / (1.0 + jnp.exp(-v))).astype(jnp.bfloat16)
+        u = values.astype(jnp.float32) * half_gain + half_shift
+        return (u + u * jnp.tanh(u)).astype(jnp.bfloat16)
 
     def place(line, values):
         for dy in range(3):
@@ -681,7 +769,7 @@
             pltpu.VMEM((n // 2, chunks, 2, CHUNK, channels), bf16),
             pltpu.VMEM((4, channels, channels), bf16),
             pltpu.VMEM((3, 3, channels, channels), bf16),
-            pltpu.VMEM((channels, channels), bf16),
+            pltpu.VMEM((128, 128), bf16),
             pltpu.VMEM((2, n, 2, channels), f32),
             pltpu.VMEM((2 * rows, channels), bf16),
             *[pltpu.VMEM((2 * rows, 128), f32)] * 3,
@@ -691,7 +779,7 @@
             pltpu.VMEM((rows, 3 * channels), bf16),
             dma,
             dma((2,)),
-            dma((5,)),
+            dma((8,)),
             dma((n // 2, chunks, 2)),
             dma((2,)),
             dma((2,)),

time: 46.8 us -> 46.5 us (level)
  no operation moved by 1% of the time
where the time goes in v5:
time: 46.5 us; the launch traced here: 46.1 us
  Pallas kernels  45.3 us (97%)
  local copies, waits for them, and re-layouts  0.8 us (2%)
    pallas_call x1, Pallas kernels, local(): pl.pallas_call(functools.partial(kernel, n, relief, wide), out_shape=pltp...  45.3 us

profile of v5, /device:TPU:0, one launch (start us, length us, event | category | flops | bytes accessed | tf_op | source)
XLA Modules:
  0.0 46.1 jit_solution(4003212543832205074)
XLA Ops:
  0.0 45.3 %shard_map.109 = bf16[512,512]{1,0:T(8,128)(2,1)S(1)} custom-call(bf16[4,128,512]{2,1,0:T(8,128)(2,1)} %latent.1, bf16[512,512]{1,0:T(8,128)(2,1)} %w_query.1, bf16[512,512]{1,0:T(8,128)(2,1)} %w_key.1, bf16[512,512]{1,0:T(8,128)(2,1)} %w_value.1, bf16[512,512]{1,0:T(8,128)(2,1)} %w_out.1, bf16[3,3,512,512]{3,2,1,0:T(8,128)(2,1)} %w_conv.1, ...), custom_call_target="tpu_custom_call" | custom-call | tf_op jit(solution)/shard_map/pallas_call | solution.py:762
  45.3 0.8 %copy.13 = bf16[4,128,512]{2,1,0:T(8,128)(2,1)} copy(bf16[4,128,512]{2,1,0:T(8,128)(2,1)S(1)} %bitcast.6) | data formatting | bytes 1048576
